TPU v7x, 128 devices: a whole 4x4x4 slice. The times are simulated.
128 devices in a mesh: gx: 4 (over x), gy: 2 (over z_hi), gz: 16 (over y, z_lo, core).
Axes of the slice: x: 4, y: 4, z: 4 (z_hi: 2, z_lo: 2; z = z_hi * 2 + z_lo), core: 2. Of those that a mesh axis runs over, the one named last changes fastest.
Arguments:
- points: float32 [3, 524288], P(None, ('gx', 'gy', 'gz')), may hold values from 0 to 1
- charges: bfloat16 [8, 524288], P(None, ('gx', 'gy', 'gz')), may hold values from -6 to 6
- arrival_order: int32 [128, 4096], P(('gx', 'gy', 'gz')), may hold values from 0 to 4095, each once within a row
- counts: int32 [128], P(('gx', 'gy', 'gz')), may hold values from 1 to 4096, 393216 in all
- basis_rows: bfloat16 [7, 524288, 128], P(None, ('gx', 'gy', 'gz')), may hold values from -6 to 6
- skeletons: float32 [3, 256, 128], replicated, may hold values from 0 to 1
Outputs:
- result: float32 [8, 524288], P(None, ('gx', 'gy', 'gz'))
Inputs may be any that keep to these rules, and one draw needn't show every extreme that they name: `arrival_order`: each row is a permutation of 0 to 4095. The counts sum to 393216, and some leaf is full.
All inputs are finite; a program needn't handle non-finite values.
Results may differ from a plain program's by a relative error of at most 0.0046.
Values sent between devices are 32-bit elements; how exact they have to be, the bound alone decides.
No kernel may reach another device: no remote copies, remote signals or barrier semaphores. Data moves between devices by JAX's collectives and lax.ppermute only.
A program may use at most 64 MiB of HBM per device.

v0:
```python
import math

import jax
import jax.numpy as jnp
from jax import lax
from jax.sharding import PartitionSpec as P

kernel_width = 0.1
dense_gain = 4.0
expand_gain = 0.25


def copy_for_each(x, axis):
    count = lax.axis_size(axis)
    return lax.all_to_all(jnp.broadcast_to(x[None], (count, *x.shape)), axis, 0, 0, tiled=True)


def joined_along(blocks, dim):
    blocks = jnp.moveaxis(blocks, 0, dim)
    dims = blocks.shape
    return blocks.reshape(*dims[:dim], dims[dim] * dims[dim + 1], *dims[dim + 2 :])


def gather_directly(x, axis, dim):
    blocks = copy_for_each(x, axis)
    return joined_along(blocks, dim)


def partner_2(block, axis, stride):
    count = lax.axis_size(axis)
    route = []
    for low in range(count):
        high = low | 1 << stride
        if high != low and high < count:
            route += [(low, high), (high, low)]
    return lax.ppermute(block, axis, route)


def squared_gap(left_pts, right_pts):
    gap_a = left_pts[0] - right_pts[0]
    gap_b = left_pts[1] - right_pts[1]
    gap_c = left_pts[2] - right_pts[2]
    return gap_a * gap_a + gap_b * gap_b + gap_c * gap_c


def butterfly(values, bit_count, swapper):
    sibling_list = []
    for bit_no in range(bit_count):
        received = swapper(values, bit_no)
        parent_sum = values[0] + received[0]
        sibling_list.append(parent_sum - values[0])
        values = values[1:] + received[1:]
    return (values, sibling_list)


def group_sums(gathered, own_index, bit_count):
    group_size = gathered.shape[0]
    member = jnp.arange(group_size, dtype=jnp.int32)
    sibling_list = []
    for bit_no in range(bit_count):
        partner = jnp.bitwise_xor(jnp.right_shift(own_index, bit_no), 1)
        selector = jnp.right_shift(member, bit_no) == partner
        picked = jnp.where(
            selector[:, None, None], gathered[:, bit_no], jnp.zeros_like(gathered[:, bit_no])
        )
        sibling_list.append(jnp.sum(picked, axis=0))
    return (sibling_list, jnp.sum(gathered[:, bit_count:], axis=0))


def per_device(points, charges, arrival_order, counts, basis_rows, skeletons):
    size_gx = lax.axis_size("gx")
    size_gy = lax.axis_size("gy")
    size_gz = lax.axis_size("gz")
    bits_x = size_gx.bit_length() - 1
    bits_y = size_gy.bit_length() - 1
    bits_z = size_gz.bit_length() - 1
    levels = bits_x + bits_y + bits_z
    device_count = size_gx * size_gy * size_gz
    index_x = lax.axis_index("gx")
    index_y = lax.axis_index("gy")
    index_z = lax.axis_index("gz")
    device = index_x * (size_gy * size_gz) + index_y * size_gz + index_z
    rhs_count = charges.shape[0]
    leaf_size = charges.shape[1]
    rank_size = basis_rows.shape[2]
    tree_charges = jnp.take(charges, arrival_order[0], axis=1)
    alive_mask = jnp.arange(leaf_size, dtype=jnp.int32) < counts[0]
    live_charges = jnp.where(alive_mask[None, :], tree_charges, jnp.zeros_like(tree_charges))
    level_scale = jnp.array(
        [2.0 ** (-0.5 * height) / math.sqrt(leaf_size) for height in range(levels)], jnp.float32
    )
    projection = (
        jnp.einsum("kp,lpr->lkr", live_charges, basis_rows, preferred_element_type=jnp.float32)
        * level_scale[:, None, None]
    )
    gathered = gather_directly(projection[None], "gz", 0)
    sibling_low, totals = group_sums(gathered, index_z, bits_z)

    def swap_mid(values, bit_no):
        return partner_2(values, "gy", bit_no)

    def swap_top(values, bit_no):
        return partner_2(values, "gx", bit_no)

    totals, sibling_mid = butterfly(totals, bits_y, swap_mid)
    leftover, sibling_top = butterfly(totals, bits_x, swap_top)
    sibling_high = sibling_mid + sibling_top
    sibling = jnp.stack(sibling_low + sibling_high)
    sibling_rounded = sibling.astype(jnp.bfloat16)
    node_ids = jnp.right_shift(device_count + device, jnp.arange(levels, dtype=jnp.int32))
    own_pts = jnp.take(skeletons, node_ids, axis=1)
    far_pts = jnp.take(skeletons, jnp.bitwise_xor(node_ids, 1), axis=1)
    distance = squared_gap(far_pts[:, :, :, None], own_pts[:, :, None, :])
    coupling = jnp.exp(-distance / kernel_width).astype(jnp.bfloat16)
    coupled = jnp.einsum(
        "lkc,lca->lka", sibling_rounded, coupling, preferred_element_type=jnp.float32
    ).astype(jnp.bfloat16)
    far_field = jnp.einsum(
        "lka,lpa->kp", coupled, basis_rows, preferred_element_type=jnp.float32
    ) * (expand_gain / math.sqrt(rank_size))
    block_size = min(1024, leaf_size)
    offsets = jnp.arange(leaf_size // block_size, dtype=jnp.int32) * block_size

    def near_block(offset):
        column_pts = lax.dynamic_slice_in_dim(points, offset, block_size, 1)
        gaps = squared_gap(points[:, :, None], column_pts[:, None, :])
        kernel = jnp.exp(-gaps / kernel_width).astype(jnp.bfloat16)
        return jnp.dot(live_charges, kernel, preferred_element_type=jnp.float32)

    near_field = lax.map(near_block, offsets)
    near_field = jnp.transpose(near_field, (1, 0, 2)).reshape(rhs_count, leaf_size)
    total = dense_gain / math.sqrt(leaf_size) * near_field + far_field
    return jnp.where(alive_mask[None, :], total, jnp.zeros_like(total))


def solution(mesh):
    placed = (
        P(None, ("gx", "gy", "gz")),
        P(None, ("gx", "gy", "gz")),
        P(("gx", "gy", "gz"), None),
        P(("gx", "gy", "gz")),
        P(None, ("gx", "gy", "gz"), None),
        P(),
    )
    return jax.shard_map(
        per_device,
        mesh=mesh,
        in_specs=placed,
        out_specs=P(None, ("gx", "gy", "gz")),
        check_vma=False,
    )
```

profile of v0, /device:TPU:12, one launch (start us, length us, event | category | flops | bytes accessed | tf_op | source)
XLA Modules:
  0.0 90.5 jit_solution(18227952873732697573)
XLA Ops:
  0.7 1.3 %copy.14 = bf16[8,4096]{0,1:T(8,128)(2,1)S(1)} copy(bf16[8,4096]{1,0:T(8,128)(2,1)} %param.12) | data formatting | bytes 131072 | tf_op args[1]
  2.0 0.7 compare_select_fusion
  2.8 0.7 iota_compare_fusion
  3.5 12.1 %gather_fusion = bf16[4096,8]{1,0:T(8,128)(2,1)S(1)} fusion(bf16[8,4096]{0,1:T(8,128)(2,1)S(1)} %copy.14, s32[4096]{0:T(1024)S(1)} %broadcast_clamp_fusion), kind=kCustom, calls=%fused_computation.2 | custom fusion | bytes 147456 | tf_op jit(solution)/shard_map/jit(_take)/gather | solution.py:86
  15.7 6.7 %fusion.7 = f32[7,8,128]{2,1,0:T(8,128)S(1)} fusion(bf16[7,4096,128]{2,1,0:T(8,128)(2,1)} %param.15, f32[7]{0:T(128)} %constant.90.clone, bf16[4096,8]{1,0:T(8,128)(2,1)S(1)} %gather_fusion, pred[4096]{0:T(1024)(128)(4,1)S(1)} %get-tuple-element.77, pred[4096]{0:T(1024)(128)(4,1)S(1)} %get-tuple-element.78), kind=kOutput, calls=%fused_computation.14 | convolution fusion | flops 58792960 | bytes 7442460 | tf_op jit(solution)/shard_map/kp,lpr->lkr/dot_general | solution.py:93
  22.4 0.8 broadcast_in_dim.91
  23.2 6.3 %all-to-all-start = ((f32[16,1,7,8,128]{4,3,2,1,0:T(8,128)}), f32[16,1,7,8,128]{4,3,2,1,0:T(8,128)S(1)}, u32[]{:S(2)}, u32[]{:S(2)}) async-start(f32[16,1,7,8,128]{4,3,2,1,0:T(8,128)} %broadcast_in_dim.91), calls=%async_computation | async-start | bytes 917504 | tf_op jit(solution)/shard_map/all_to_all | solution.py:15
  29.5 1.4 %fusion.36 = bf16[8,4096]{0,1:T(8,128)(2,1)S(1)} fusion(bf16[4096,8]{1,0:T(8,128)(2,1)S(1)} %gather_fusion, pred[4096]{0:T(1024)(128)(4,1)S(1)} %get-tuple-element.78, pred[4096]{0:T(1024)(128)(4,1)S(1)} %get-tuple-element.77), kind=kLoop, calls=%fused_computation.81 | loop fusion | flops 65536 | bytes 139264 | tf_op jit(solution)/shard_map/jit(_where)/select_n | solution.py:88
  31.0 0.6 gather_fusion.1
  32.5 37.4 %while.10 = (s32[]{:T(128)}, f32[4,8,1024]{2,1,0:T(8,128)S(1)}, f32[3,4096]{1,0:T(4,128)S(1)}, s32[4]{0:T(128)S(1)}, bf16[8,4096]{1,0:T(8,128)(2,1)S(1)}, /*index=5*/s32[]{:T(128)}, s32[]{:T(128)}, s32[]{:T(128)}, s32[]{}, s32[]{}) while((s32[]{:T(128)}, f32[4,8,1024]{2,1,0:T(8,128)S(1)}, f32[3,4096]{1,0:T(4,128)S(1)}, s32[4]{0:T(128)S(1)}, ...), condition=%wide.region_1.2_spmd, body=%wide.region_0.1_spmd.sunk | while | flops 113246216 | bytes 282811 | solution.py:130
  32.5 0.7 dynamic_slice.8
  35.4 6.4 %fusion.47 = f32[4,8,1024]{2,1,0:T(8,128)S(1)} fusion(f32[4,8,1024]{2,1,0:T(8,128)S(1)} %get-tuple-element.139, s32[]{:T(128)} %get-tuple-element.138, bf16[8,4096]{1,0:T(8,128)(2,1)S(1)} %get-tuple-element.152, f32[1024]{0:T(1024)S(1)} %bitcast.122, f32[4096]{0:T(1024)S(1)} %bitcast.118, f32[1024]{0:T(1024)S(1)} %bitcast.121, ...), kind=kOutput, calls=%fused_computation.6.clone.1 | convolution fusion | flops 113246208 | bytes 159748 | tf_op jit(solution)/shard_map/while/body/eval_jaxpr/dot_general | solution.py:128
  41.9 0.7 dynamic_slice.8
  44.7 6.4 %fusion.47 = f32[4,8,1024]{2,1,0:T(8,128)S(1)} fusion(f32[4,8,1024]{2,1,0:T(8,128)S(1)} %get-tuple-element.139, s32[]{:T(128)} %get-tuple-element.138, bf16[8,4096]{1,0:T(8,128)(2,1)S(1)} %get-tuple-element.152, f32[1024]{0:T(1024)S(1)} %bitcast.122, f32[4096]{0:T(1024)S(1)} %bitcast.118, f32[1024]{0:T(1024)S(1)} %bitcast.121, ...), kind=kOutput, calls=%fused_computation.6.clone.1 | convolution fusion | flops 113246208 | bytes 159748 | tf_op jit(solution)/shard_map/while/body/eval_jaxpr/dot_general | solution.py:128
  51.2 0.7 dynamic_slice.8
  54.1 6.4 %fusion.47 = f32[4,8,1024]{2,1,0:T(8,128)S(1)} fusion(f32[4,8,1024]{2,1,0:T(8,128)S(1)} %get-tuple-element.139, s32[]{:T(128)} %get-tuple-element.138, bf16[8,4096]{1,0:T(8,128)(2,1)S(1)} %get-tuple-element.152, f32[1024]{0:T(1024)S(1)} %bitcast.122, f32[4096]{0:T(1024)S(1)} %bitcast.118, f32[1024]{0:T(1024)S(1)} %bitcast.121, ...), kind=kOutput, calls=%fused_computation.6.clone.1 | convolution fusion | flops 113246208 | bytes 159748 | tf_op jit(solution)/shard_map/while/body/eval_jaxpr/dot_general | solution.py:128
  60.5 0.7 dynamic_slice.8
  63.4 6.4 %fusion.47 = f32[4,8,1024]{2,1,0:T(8,128)S(1)} fusion(f32[4,8,1024]{2,1,0:T(8,128)S(1)} %get-tuple-element.139, s32[]{:T(128)} %get-tuple-element.138, bf16[8,4096]{1,0:T(8,128)(2,1)S(1)} %get-tuple-element.152, f32[1024]{0:T(1024)S(1)} %bitcast.122, f32[4096]{0:T(1024)S(1)} %bitcast.118, f32[1024]{0:T(1024)S(1)} %bitcast.121, ...), kind=kOutput, calls=%fused_computation.6.clone.1 | convolution fusion | flops 113246208 | bytes 159748 | tf_op jit(solution)/shard_map/while/body/eval_jaxpr/dot_general | solution.py:128
  70.2 3.7 %collective-permute-start = (f32[3,8,128]{2,1,0:T(8,128)S(1)}, f32[3,8,128]{2,1,0:T(8,128)S(1)}, u32[]{:S(2)}, u32[]{:S(2)}) collective-permute-start(f32[3,8,128]{2,1,0:T(8,128)S(1)} %slice_reduce_fusion), channel_id=1, source_target_pairs={{0,16},{16,0},{1,17},{17,1},{2,18},{18,2},{3,19},{19,3},{4,20},{20... | collective-permute-start | bytes 36872 | tf_op jit(solution)/shard_map/ppermute | solution.py:36
  73.9 1.7 %collective-permute-done = f32[3,8,128]{2,1,0:T(8,128)S(1)} collective-permute-done((f32[3,8,128]{2,1,0:T(8,128)S(1)}, f32[3,8,128]{2,1,0:T(8,128)S(1)}, u32[]{:S(2)}, u32[]{:S(2)}) %collective-permute-start) | collective-permute-done | bytes 12320 | tf_op jit(solution)/shard_map/ppermute | solution.py:36
  75.5 1.2 %collective-permute-start.1 = (f32[2,8,128]{2,1,0:T(8,128)S(1)}, f32[2,8,128]{2,1,0:T(8,128)S(1)}, u32[]{:S(2)}, u32[]{:S(2)}) collective-permute-start(f32[2,8,128]{2,1,0:T(8,128)S(1)} %slice_add_fusion), channel_id=1, source_target_pairs={{0,32},{32,0},{64,96},{96,64},{1,33},{33,1},{65,97},{97,65},{2,34}... | collective-permute-start | bytes 24584 | tf_op jit(solution)/shard_map/ppermute | solution.py:36
  76.7 2.4 %collective-permute-done.1 = f32[2,8,128]{2,1,0:T(8,128)S(1)} collective-permute-done((f32[2,8,128]{2,1,0:T(8,128)S(1)}, f32[2,8,128]{2,1,0:T(8,128)S(1)}, u32[]{:S(2)}, u32[]{:S(2)}) %collective-permute-start.1) | collective-permute-done | bytes 8224 | tf_op jit(solution)/shard_map/ppermute | solution.py:36
  79.7 4.6 %collective-permute-done.2 = f32[1,8,128]{2,1,0:T(8,128)S(1)} collective-permute-done((f32[1,8,128]{2,1,0:T(8,128)S(1)}, f32[1,8,128]{2,1,0:T(8,128)S(1)}, u32[]{:S(2)}, u32[]{:S(2)}) %collective-permute-start.2) | collective-permute-done | bytes 4128 | tf_op jit(solution)/shard_map/ppermute | solution.py:36
  84.3 6.2 %fusion.6 = f32[8,4096]{1,0:T(8,128)} fusion(f32[8,4096]{1,0:T(8,128)S(1)} %bitcast.116, bf16[7,4096,128]{2,1,0:T(8,128)(2,1)} %param.15, bf16[7,8,128]{2,1,0:T(8,128)(2,1)S(1)} %constant_dynamic-update-slice_fusion, f32[7,128]{1,0:T(8,128)S(1)} %get-tuple-element.73, f32[7,128]{1,0:T(8,128)S(1)} %get-tuple-element.70, f32[7,128]{1,0:T(8,128)S(1)} %get-tuple-element.74, ...), kind=kOutput, calls=%fused_computation.12 | convolution fusion | flops 61922304 | bytes 7642112 | tf_op jit(solution)/shard_map/lka,lpa->kp/dot_general | solution.py:118
  (41 shorter events, 2.4 us)
Async XLA Ops:
  0.0 31.0 %copy-start = (f32[3,256,128]{2,1,0:T(8,128)S(1)}, f32[3,256,128]{2,1,0:T(8,128)}, u32[]{:S(2)}) copy-start(f32[3,256,128]{2,1,0:T(8,128)} %param.16) | copy-start | bytes 1179652
  15.7 16.8 %copy-start.1 = (f32[3,4096]{1,0:T(4,128)S(1)}, f32[3,4096]{1,0:T(4,128)}, u32[]{:S(2)}) copy-start(f32[3,4096]{1,0:T(4,128)} %param.11) | copy-start | bytes 147460
  23.2 46.8 %all-to-all-start = ((f32[16,1,7,8,128]{4,3,2,1,0:T(8,128)}), f32[16,1,7,8,128]{4,3,2,1,0:T(8,128)S(1)}, u32[]{:S(2)}, u32[]{:S(2)}) async-start(f32[16,1,7,8,128]{4,3,2,1,0:T(8,128)} %broadcast_in_dim.91), calls=%async_computation | async-start | bytes 917504 | tf_op jit(solution)/shard_map/all_to_all | solution.py:15
  70.2 5.3 %collective-permute-start = (f32[3,8,128]{2,1,0:T(8,128)S(1)}, f32[3,8,128]{2,1,0:T(8,128)S(1)}, u32[]{:S(2)}, u32[]{:S(2)}) collective-permute-start(f32[3,8,128]{2,1,0:T(8,128)S(1)} %slice_reduce_fusion), channel_id=1, source_target_pairs={{0,16},{16,0},{1,17},{17,1},{2,18},{18,2},{3,19},{19,3},{4,20},{20... | collective-permute-start | bytes 36872 | tf_op jit(solution)/shard_map/ppermute | solution.py:36
  75.5 3.7 %collective-permute-start.1 = (f32[2,8,128]{2,1,0:T(8,128)S(1)}, f32[2,8,128]{2,1,0:T(8,128)S(1)}, u32[]{:S(2)}, u32[]{:S(2)}) collective-permute-start(f32[2,8,128]{2,1,0:T(8,128)S(1)} %slice_add_fusion), channel_id=1, source_target_pairs={{0,32},{32,0},{64,96},{96,64},{1,33},{33,1},{65,97},{97,65},{2,34}... | collective-permute-start | bytes 24584 | tf_op jit(solution)/shard_map/ppermute | solution.py:36
  79.2 5.1 %collective-permute-start.2 = (f32[1,8,128]{2,1,0:T(8,128)S(1)}, f32[1,8,128]{2,1,0:T(8,128)S(1)}, u32[]{:S(2)}, u32[]{:S(2)}) collective-permute-start(f32[1,8,128]{2,1,0:T(8,128)S(1)} %slice_add_fusion.1), channel_id=1, source_target_pairs={{0,64},{64,0},{32,96},{96,32},{1,65},{65,1},{33,97},{97,33},{2,66}... | collective-permute-start | bytes 12296 | tf_op jit(solution)/shard_map/ppermute | solution.py:36
where the time goes:
time: 91.1 us; the launch traced here: 90.5 us
  matrix products  38.7 us (42%)
  local copies, waits for them, and re-layouts  19 us (21%)
  starting transfers between devices  11.6 us (13%)
  waiting for transfers between devices  8.69 us (10%)
  loops' own time  8.37 us (9%)
  other arithmetic  3.29 us (4%)
    dot_general x4, matrix products, near_block(): return jnp.dot(live_charges, kernel, preferred_element_type=jnp.float32)  25.8 us
    gather x1, local copies, waits for them, and re-layouts, per_device(): tree_charges = jnp.take(charges, arrival_order[0], axis=1)  12.1 us
    ppermute x3, waiting for transfers between devices, partner_2(): return lax.ppermute(block, axis, route)  8.69 us
    another operation x1, loops' own time, per_device(): near_field = lax.map(near_block, offsets)  8.37 us
    dot_general x1, matrix products, per_device(): jnp.einsum('kp,lpr->lkr', live_charges, basis_rows, preferred_element_typ...  6.7 us
    all_to_all x1, starting transfers between devices, copy_for_each(): lax.all_to_all(jnp.broadcast_to(x[None], (count, *x.shape)), axis, 0, 0,...  6.29 us
    dot_general x1, matrix products, per_device(): jnp.einsum('lka,lpa->kp', coupled, basis_rows, preferred_element_type=jnp...  6.18 us
    ppermute x3, starting transfers between devices, partner_2(): return lax.ppermute(block, axis, route)  5.36 us
  transfers between devices with their start and end apart: 4, of which 3 were waited for; matrix products, arithmetic and copies ran while one was open for 35% of the time, Pallas kernels for 0%

commit v1 on v0

v1 whole, which is shorter than its diff:
```python
import math

import jax
import jax.numpy as jnp
from jax import lax
from jax.experimental import pallas as pl
from jax.experimental.pallas import tpu as pltpu
from jax.sharding import PartitionSpec as P

kernel_width = 0.1
dense_gain = 4.0
expand_gain = 0.25
axes = ("gx", "gy", "gz")
log2_rate = math.log2(math.e) / kernel_width


def device_index():
    size_y = lax.axis_size("gy")
    size_z = lax.axis_size("gz")
    return (lax.axis_index("gx") * size_y + lax.axis_index("gy")) * size_z + lax.axis_index("gz")


def head_kernel(scal_ref, order_ref, charges_ref, basis_ref, live_ref, send_ref, table_ref, acc_ref):
    step = pl.program_id(0)
    levels, rows, rank = basis_ref.shape
    rhs, leaf = charges_ref.shape
    high = leaf // 128

    @pl.when(step == 0)
    def _():
        wide = charges_ref[...].astype(jnp.float32)
        table_ref[...] = jnp.concatenate(
            [wide[:, h * 128 : (h + 1) * 128] for h in range(high)], axis=0
        ).astype(jnp.bfloat16)
        acc_ref[...] = jnp.zeros_like(acc_ref)

    order = order_ref[...]
    low_part = jnp.bitwise_and(order, 127)
    high_part = jnp.right_shift(order, 7)
    lane_of = lax.broadcasted_iota(jnp.int32, (128, rows), 0)
    one_hot = jnp.where(lane_of == low_part, 1.0, 0.0).astype(jnp.bfloat16)
    spread = jnp.dot(table_ref[...], one_hot, preferred_element_type=jnp.float32)
    high_part = jnp.broadcast_to(high_part, (rhs, rows))
    picked = jnp.zeros((rhs, rows), jnp.float32)
    for h in range(high):
        picked = jnp.where(high_part == h, spread[h * rhs : (h + 1) * rhs], picked)
    slot = lax.broadcasted_iota(jnp.int32, (rhs, rows), 1) + step * rows
    live = jnp.where(slot < scal_ref[0], picked, 0.0).astype(jnp.bfloat16)
    live_ref[...] = live
    basis = jnp.concatenate([basis_ref[l] for l in range(levels)], axis=1)
    acc_ref[...] += jnp.dot(live, basis, preferred_element_type=jnp.float32)

    @pl.when(step == pl.num_programs(0) - 1)
    def _():
        own = scal_ref[1]
        for l in range(levels):
            scale = 2.0 ** (-0.5 * l) / math.sqrt(leaf)
            block = acc_ref[:, l * rank : (l + 1) * rank] * scale
            first = jnp.bitwise_xor(own >> l, 1) << l
            for i in range(1 << l):
                send_ref[first + i] = block
        send_ref[own] = jnp.zeros((rhs, rank), jnp.float32)


def head(scal, order, charges, basis):
    levels, leaf, rank = basis.shape
    rhs = charges.shape[0]
    rows = min(512, leaf)
    return pl.pallas_call(
        head_kernel,
        grid=(leaf // rows,),
        in_specs=[
            pl.BlockSpec(memory_space=pltpu.SMEM),
            pl.BlockSpec((1, rows), lambda i: (0, i)),
            pl.BlockSpec((rhs, leaf), lambda i: (0, 0)),
            pl.BlockSpec((levels, rows, rank), lambda i: (0, i, 0)),
        ],
        out_specs=[
            pl.BlockSpec((rhs, rows), lambda i: (0, i)),
            pl.BlockSpec((1 << levels, rhs, rank), lambda i: (0, 0, 0)),
        ],
        out_shape=[
            jax.ShapeDtypeStruct((rhs, leaf), jnp.bfloat16),
            jax.ShapeDtypeStruct((1 << levels, rhs, rank), jnp.float32),
        ],
        scratch_shapes=[
            pltpu.VMEM((leaf // 128 * rhs, 128), jnp.bfloat16),
            pltpu.VMEM((rhs, levels * rank), jnp.float32),
        ],
        compiler_params=pltpu.CompilerParams(vmem_limit_bytes=24 << 20),
        name="head",
    )(scal, order, charges, basis)


def bf16_pieces(x):
    pieces = []
    for _ in range(3):
        piece = x.astype(jnp.bfloat16).astype(jnp.float32)
        pieces.append(piece)
        x = x - piece
    return pieces


def near_kernel(scal_ref, points_ref, live_ref, skel_ref, near_ref, coup_ref, tall_ref, wide_ref, spare_ref):
    step = pl.program_id(0)
    rhs, leaf = live_ref.shape
    columns = near_ref.shape[1]
    rows = min(512, leaf)

    @pl.when(step == 0)
    def _():
        scaled = (points_ref[...] - 0.5) * math.sqrt(2.0 * log2_rate)
        high, mid, low = bf16_pieces(scaled)
        norm = jnp.sum(scaled * scaled, axis=0, keepdims=True) * -0.5
        norms = jnp.concatenate(bf16_pieces(norm), axis=0)
        ones = jnp.ones_like(norms)
        spare_ref[...] = jnp.zeros_like(spare_ref)
        for at, piece in ((0, high), (3, norms), (8, mid), (11, ones), (16, low), (24, high), (32, mid), (40, high)):
            spare_ref[at : at + 3, :] = piece
        for b in range(leaf // 128):
            tall_ref[b * 128 : (b + 1) * 128, :] = spare_ref[:, b * 128 : (b + 1) * 128].T.astype(jnp.bfloat16)
        for at, piece in ((0, high), (3, ones), (8, high), (11, norms), (16, high), (24, mid), (32, mid), (40, low)):
            spare_ref[at : at + 3, :] = piece
        wide_ref[...] = spare_ref[...].astype(jnp.bfloat16)

        own = scal_ref[1]
        devices = 1 << coup_ref.shape[0]
        for l in range(coup_ref.shape[0]):
            node = (devices + own) >> l
            gap = None
            for axis in range(3):
                mine = skel_ref[axis, pl.ds(node, 1), :]
                other = skel_ref[axis, pl.ds(jnp.bitwise_xor(node, 1), 1), :]
                other = jnp.broadcast_to(other, (other.shape[1], other.shape[1])).T
                diff = other - mine
                gap = diff * diff if gap is None else gap + diff * diff
            coup_ref[l] = jnp.exp2(gap * -log2_rate).astype(jnp.bfloat16)

    column = wide_ref[:, pl.ds(pl.multiple_of(step * columns, 128), columns)]
    total = jnp.zeros((rhs, columns), jnp.float32)
    for at in range(0, leaf, rows):
        power = jnp.dot(tall_ref[at : at + rows, :], column, preferred_element_type=jnp.float32)
        kernel = jnp.exp2(power).astype(jnp.bfloat16)
        total += jnp.dot(live_ref[:, at : at + rows], kernel, preferred_element_type=jnp.float32)
    near_ref[...] = total


def near(scal, points, live, skeletons, levels):
    rhs, leaf = live.shape
    rank = skeletons.shape[2]
    columns = min(256, leaf)
    return pl.pallas_call(
        near_kernel,
        grid=(leaf // columns,),
        in_specs=[
            pl.BlockSpec(memory_space=pltpu.SMEM),
            pl.BlockSpec((3, leaf), lambda i: (0, 0)),
            pl.BlockSpec((rhs, leaf), lambda i: (0, 0)),
            pl.BlockSpec(skeletons.shape, lambda i: (0, 0, 0)),
        ],
        out_specs=[
            pl.BlockSpec((rhs, columns), lambda i: (0, i)),
            pl.BlockSpec((levels, rank, rank), lambda i: (0, 0, 0)),
        ],
        out_shape=[
            jax.ShapeDtypeStruct((rhs, leaf), jnp.float32),
            jax.ShapeDtypeStruct((levels, rank, rank), jnp.bfloat16),
        ],
        scratch_shapes=[
            pltpu.VMEM((leaf, 48), jnp.bfloat16),
            pltpu.VMEM((48, leaf), jnp.bfloat16),
            pltpu.VMEM((48, leaf), jnp.float32),
        ],
        compiler_params=pltpu.CompilerParams(vmem_limit_bytes=24 << 20),
        cost_estimate=pl.CostEstimate(flops=4 << 30, bytes_accessed=1 << 20, transcendentals=leaf * leaf),
        name="near",
    )(scal, points, live, skeletons)


def tail_kernel(scal_ref, got_ref, coup_ref, near_ref, basis_ref, out_ref, coupled_ref):
    step = pl.program_id(0)
    levels, rows, rank = basis_ref.shape
    rhs = near_ref.shape[0]
    leaf = rows * pl.num_programs(0)

    @pl.when(step == 0)
    def _():
        own = scal_ref[1]
        for l in range(levels):
            first = jnp.bitwise_xor(own >> l, 1) << l
            sums = [got_ref[first + i] for i in range(1 << l)]
            while len(sums) > 1:
                sums = [a + b for a, b in zip(sums[::2], sums[1::2])]
            coupled = jnp.dot(sums[0].astype(jnp.bfloat16), coup_ref[l], preferred_element_type=jnp.float32)
            coupled_ref[:, l * rank : (l + 1) * rank] = coupled.astype(jnp.bfloat16)

    basis = jnp.concatenate([basis_ref[l] for l in range(levels)], axis=1)
    far = lax.dot_general(
        coupled_ref[...], basis, (((1,), (1,)), ((), ())), preferred_element_type=jnp.float32
    )
    total = dense_gain / math.sqrt(leaf) * near_ref[...] + far * (expand_gain / math.sqrt(rank))
    slot = lax.broadcasted_iota(jnp.int32, (rhs, rows), 1) + step * rows
    out_ref[...] = jnp.where(slot < scal_ref[0], total, 0.0)


def tail(scal, got, coup, near_field, basis):
    levels, leaf, rank = basis.shape
    rhs = near_field.shape[0]
    rows = min(512, leaf)
    return pl.pallas_call(
        tail_kernel,
        grid=(leaf // rows,),
        in_specs=[
            pl.BlockSpec(memory_space=pltpu.SMEM),
            pl.BlockSpec(got.shape, lambda i: (0, 0, 0)),
            pl.BlockSpec(coup.shape, lambda i: (0, 0, 0)),
            pl.BlockSpec((rhs, rows), lambda i: (0, i)),
            pl.BlockSpec((levels, rows, rank), lambda i: (0, i, 0)),
        ],
        out_specs=pl.BlockSpec((rhs, rows), lambda i: (0, i)),
        out_shape=jax.ShapeDtypeStruct((rhs, leaf), jnp.float32),
        scratch_shapes=[pltpu.VMEM((rhs, levels * rank), jnp.bfloat16)],
        compiler_params=pltpu.CompilerParams(vmem_limit_bytes=24 << 20),
        name="tail",
    )(scal, got, coup, near_field, basis)


def per_device(points, charges, arrival_order, counts, basis_rows, skeletons):
    scal = jnp.stack([counts[0], device_index()])
    live, send = head(scal, arrival_order, charges, basis_rows)
    got = lax.all_to_all(send, axes, 0, 0, tiled=True)
    near_field, coup = near(scal, points, live, skeletons, basis_rows.shape[0])
    return tail(scal, got, coup, near_field, basis_rows)


def solution(mesh):
    placed = (
        P(None, axes),
        P(None, axes),
        P(axes, None),
        P(axes),
        P(None, axes, None),
        P(),
    )
    return jax.shard_map(
        per_device,
        mesh=mesh,
        in_specs=placed,
        out_specs=P(None, axes),
        check_vma=False,
    )
```

time: 91.1 us -> 52.1 us (0.57)
  the two profiles are of different devices: /device:TPU:12 before, /device:TPU:1 now
where the time goes in v1:
time: 52.1 us; the launch traced here: 51.7 us
  Pallas kernels  31.7 us (61%)
  starting transfers between devices  11.5 us (22%)
  local copies, waits for them, and re-layouts  7.75 us (15%)
  between operations  0.69 us (1%)
    pallas_call x1, Pallas kernels, near(): pl.pallas_call(near_kernel, grid=(leaf // columns,), in_specs=[pl.BlockSp...  21.2 us
    all_to_all x1, starting transfers between devices, per_device(): got = lax.all_to_all(send, axes, 0, 0, tiled=True)  11.5 us
    unnamed x12, local copies, waits for them, and re-layouts  7.75 us
    pallas_call x1, Pallas kernels, head(): pl.pallas_call(head_kernel, grid=(leaf // rows,), in_specs=[pl.BlockSpec(...  5.29 us
    pallas_call x1, Pallas kernels, tail(): pl.pallas_call(tail_kernel, grid=(leaf // rows,), in_specs=[pl.BlockSpec(...  5.23 us
  transfers between devices with their start and end apart: 1, of which 0 were waited for; matrix products, arithmetic and copies ran while one was open for 0% of the time, Pallas kernels for 41%

profile of v1, /device:TPU:1, one launch (start us, length us, event | category | flops | bytes accessed | tf_op | source)
XLA Modules:
  0.0 51.7 jit_solution(7519061255239836770)
XLA Ops:
  0.7 0.1 pad_add_fusion.scal_ref
  0.7 0.0 copy-start
  0.7 3.1 %copy-done = bf16[7,4096,128]{2,1,0:T(8,128)(2,1)S(1)} copy-done((bf16[7,4096,128]{2,1,0:T(8,128)(2,1)S(1)}, bf16[7,4096,128]{2,1,0:T(8,128)(2,1)}, u32[]{:S(2)}) %copy-start) | copy-done | bytes 7340056
  3.8 0.0 copy-start.2
  3.8 0.8 %copy-done.2 = bf16[8,4096]{1,0:T(8,128)(2,1)S(1)} copy-done((bf16[8,4096]{1,0:T(8,128)(2,1)S(1)}, bf16[8,4096]{1,0:T(8,128)(2,1)}, u32[]{:S(2)}) %copy-start.2) | copy-done | bytes 65560
  4.7 0.0 copy-start.3
  4.7 0.7 %copy-done.3 = s32[1,4096]{1,0:T(1,128)S(1)} copy-done((s32[1,4096]{1,0:T(1,128)S(1)}, s32[1,4096]{1,0:T(1,128)}, u32[]{:S(2)}) %copy-start.3) | copy-done | bytes 16408
  5.4 0.0 copy-start.4
  5.4 0.0 copy-start.5
  5.4 5.3 %head.1 = (bf16[8,4096]{1,0:T(8,128)(2,1)S(1)}, f32[128,8,128]{2,1,0:T(8,128)}) custom-call(s32[2]{0:T(128)S(1)} %pad_add_fusion.scal_ref, s32[1,4096]{1,0:T(1,128)S(1)} %copy-done.3, bf16[8,4096]{1,0:T(8,128)(2,1)S(1)} %copy-done.2, bf16[7,4096,128]{2,1,0:T(8,128)(2,1)S(1)} %copy-done), custom_call_target="tpu_custom_call" | custom-call | tf_op jit(solution)/shard_map/head/pallas_call | solution.py:69
  10.7 11.5 %all-to-all-start = ((f32[128,8,128]{2,1,0:T(8,128)}), f32[128,8,128]{2,1,0:T(8,128)S(1)}, u32[]{:S(2)}, u32[]{:S(2)}) async-start(f32[128,8,128]{2,1,0:T(8,128)} %get-tuple-element.9), calls=%async_computation | async-start | bytes 1048576 | tf_op jit(solution)/shard_map/all_to_all | solution.py:231
  22.1 0.0 copy-done.4
  22.2 0.0 copy-done.5
  22.2 21.2 %near.1 = (f32[8,4096]{1,0:T(8,128)S(1)}, bf16[7,128,128]{2,1,0:T(8,128)(2,1)S(1)}) custom-call(s32[2]{0:T(128)S(1)} %pad_add_fusion.scal_ref, f32[3,4096]{1,0:T(4,128)S(1)} %copy-done.5, bf16[8,4096]{1,0:T(8,128)(2,1)S(1)} %get-tuple-element.10.live_ref, f32[3,256,128]{2,1,0:T(8,128)S(1)} %copy-done.4), custom_call_target="tpu_custom_call" | custom-call | flops 4294967296 | bytes 1048576 | tf_op jit(solution)/shard_map/near/pallas_call | solution.py:152
  43.4 0.0 all-to-all-done.got_ref
  43.4 0.0 copy-start.1
  43.4 3.1 %copy-done.1 = bf16[7,4096,128]{2,1,0:T(8,128)(2,1)S(1)} copy-done((bf16[7,4096,128]{2,1,0:T(8,128)(2,1)S(1)}, bf16[7,4096,128]{2,1,0:T(8,128)(2,1)}, u32[]{:S(2)}) %copy-start.1) | copy-done | bytes 7340056
  46.5 5.2 %tail.1 = f32[8,4096]{1,0:T(8,128)} custom-call(s32[2]{0:T(128)S(1)} %pad_add_fusion.scal_ref, f32[128,8,128]{2,1,0:T(8,128)S(1)} %all-to-all-done.got_ref, bf16[7,128,128]{2,1,0:T(8,128)(2,1)S(1)} %get-tuple-element.11.coup_ref, f32[8,4096]{1,0:T(8,128)S(1)} %get-tuple-element.12.near_ref, bf16[7,4096,128]{2,1,0:T(8,128)(2,1)S(1)} %copy-done.1), custom_call_target="tpu_custom_call" | custom-call | tf_op jit(solution)/shard_map/tail/pallas_call | solution.py:210
Async XLA Ops:
  0.7 3.1 %copy-start = (bf16[7,4096,128]{2,1,0:T(8,128)(2,1)S(1)}, bf16[7,4096,128]{2,1,0:T(8,128)(2,1)}, u32[]{:S(2)}) copy-start(bf16[7,4096,128]{2,1,0:T(8,128)(2,1)} %basis_ref.3) | copy-start | bytes 22020100
  3.8 0.8 %copy-start.2 = (bf16[8,4096]{1,0:T(8,128)(2,1)S(1)}, bf16[8,4096]{1,0:T(8,128)(2,1)}, u32[]{:S(2)}) copy-start(bf16[8,4096]{1,0:T(8,128)(2,1)} %charges_ref.1) | copy-start | bytes 196612
  4.7 0.7 %copy-start.3 = (s32[1,4096]{1,0:T(1,128)S(1)}, s32[1,4096]{1,0:T(1,128)}, u32[]{:S(2)}) copy-start(s32[1,4096]{1,0:T(1,128)} %order_ref.1) | copy-start | bytes 49156
  5.4 16.8 %copy-start.4 = (f32[3,256,128]{2,1,0:T(8,128)S(1)}, f32[3,256,128]{2,1,0:T(8,128)}, u32[]{:S(2)}) copy-start(f32[3,256,128]{2,1,0:T(8,128)} %skel_ref.1) | copy-start | bytes 1179652
  5.4 16.8 %copy-start.5 = (f32[3,4096]{1,0:T(4,128)S(1)}, f32[3,4096]{1,0:T(4,128)}, u32[]{:S(2)}) copy-start(f32[3,4096]{1,0:T(4,128)} %points_ref.1) | copy-start | bytes 147460
  10.7 32.7 %all-to-all-start = ((f32[128,8,128]{2,1,0:T(8,128)}), f32[128,8,128]{2,1,0:T(8,128)S(1)}, u32[]{:S(2)}, u32[]{:S(2)}) async-start(f32[128,8,128]{2,1,0:T(8,128)} %get-tuple-element.9), calls=%async_computation | async-start | bytes 1048576 | tf_op jit(solution)/shard_map/all_to_all | solution.py:231
  43.4 3.1 %copy-start.1 = (bf16[7,4096,128]{2,1,0:T(8,128)(2,1)S(1)}, bf16[7,4096,128]{2,1,0:T(8,128)(2,1)}, u32[]{:S(2)}) copy-start(bf16[7,4096,128]{2,1,0:T(8,128)(2,1)} %basis_ref.3) | copy-start | bytes 22020100

commit v2 on v0

v2 whole, which is shorter than its diff:
```python
import math

import jax
import jax.numpy as jnp
from jax import lax
from jax.experimental import pallas as pl
from jax.experimental.pallas import tpu as pltpu
from jax.sharding import PartitionSpec as P

kernel_width = 0.1
dense_gain = 4.0
expand_gain = 0.25
axes = ("gx", "gy", "gz")
log2_rate = math.log2(math.e) / kernel_width


def in_hbm(x):
    return pltpu.with_memory_space_constraint(x, pltpu.HBM)


def device_index():
    size_y = lax.axis_size("gy")
    size_z = lax.axis_size("gz")
    return (lax.axis_index("gx") * size_y + lax.axis_index("gy")) * size_z + lax.axis_index("gz")


def bf16_pieces(x):
    pieces = []
    for _ in range(3):
        piece = x.astype(jnp.bfloat16).astype(jnp.float32)
        pieces.append(piece)
        x = x - piece
    return pieces


def features(points_ref, tall_ref, wide_ref, spare_ref):
    leaf = points_ref.shape[1]
    spare_ref[...] = jnp.zeros_like(spare_ref)
    spare_ref[0:3, :] = (points_ref[...] - 0.5) * math.sqrt(2.0 * log2_rate)
    scaled = spare_ref[...]
    high, mid, _ = bf16_pieces(scaled)
    norm = jnp.sum(scaled * scaled, axis=0, keepdims=True) * -0.5
    norms = bf16_pieces(jnp.broadcast_to(norm, scaled.shape))
    row = lax.broadcasted_iota(jnp.int32, scaled.shape, 0)
    place = jnp.where(row == 3, norms[0], jnp.where(row == 4, norms[1], jnp.where(row == 5, norms[2], 0.0)))
    ones = jnp.where((row >= 3) & (row < 6), 1.0, 0.0)
    axis = row < 3
    wide = [jnp.where(axis, high, ones), jnp.where(axis, high, place), mid, mid]
    tall = [jnp.where(axis, high, place), jnp.where(axis, mid, ones), high, mid]
    wide_ref[...] = jnp.concatenate(wide, axis=0).astype(jnp.bfloat16)
    tall = jnp.concatenate(tall, axis=0)
    for b in range(leaf // 128):
        tall_ref[b * 128 : (b + 1) * 128, :] = tall[:, b * 128 : (b + 1) * 128].T.astype(jnp.bfloat16)


def head_kernel(
    scal_ref, order_hbm, charges_hbm, points_hbm, basis_hbm,
    live_ref, send_ref, tall_ref, wide_ref,
    basis_ref, order_ref, charges_ref, points_ref, table_ref, acc_ref, spare_ref, sems,
):
    levels, leaf, rank = basis_ref.shape
    rhs = charges_ref.shape[0]
    high = leaf // 128
    rows = min(512, leaf)
    steps = leaf // rows
    small = [
        pltpu.make_async_copy(charges_hbm, charges_ref, sems.at[steps]),
        pltpu.make_async_copy(order_hbm, order_ref, sems.at[steps + 1]),
        pltpu.make_async_copy(points_hbm, points_ref, sems.at[steps + 2]),
    ]
    large = [
        pltpu.make_async_copy(
            basis_hbm.at[:, pl.ds(s * rows, rows), :], basis_ref.at[:, pl.ds(s * rows, rows), :], sems.at[s]
        )
        for s in range(steps)
    ]
    for copy in small + large:
        copy.start()
    small[2].wait()
    features(points_ref, tall_ref, wide_ref, spare_ref)
    small[0].wait()
    small[1].wait()
    wide = charges_ref[...].astype(jnp.float32)
    table_ref[...] = jnp.concatenate(
        [wide[:, h * 128 : (h + 1) * 128] for h in range(high)], axis=0
    ).astype(jnp.bfloat16)
    acc_ref[...] = jnp.zeros_like(acc_ref)
    for s in range(steps):
        order = order_ref[:, s * rows : (s + 1) * rows]
        low_part = jnp.bitwise_and(order, 127)
        high_part = jnp.broadcast_to(jnp.right_shift(order, 7), (rhs, rows))
        lane_of = lax.broadcasted_iota(jnp.int32, (128, rows), 0)
        one_hot = jnp.where(lane_of == low_part, 1.0, 0.0).astype(jnp.bfloat16)
        spread = jnp.dot(table_ref[...], one_hot, preferred_element_type=jnp.float32)
        picked = jnp.zeros((rhs, rows), jnp.float32)
        for h in range(high):
            picked = jnp.where(high_part == h, spread[h * rhs : (h + 1) * rhs], picked)
        slot = lax.broadcasted_iota(jnp.int32, (rhs, rows), 1) + s * rows
        live = jnp.where(slot < scal_ref[0], picked, 0.0).astype(jnp.bfloat16)
        live_ref[:, s * rows : (s + 1) * rows] = live
    for s in range(steps):
        large[s].wait()
        live = live_ref[:, s * rows : (s + 1) * rows]
        basis = jnp.concatenate([basis_ref[l, s * rows : (s + 1) * rows, :] for l in range(levels)], axis=1)
        acc_ref[...] += jnp.dot(live, basis, preferred_element_type=jnp.float32)
    own = scal_ref[1]
    for l in range(levels):
        scale = 2.0 ** (-0.5 * l) / math.sqrt(leaf)
        block = acc_ref[:, l * rank : (l + 1) * rank] * scale
        first = jnp.bitwise_xor(own >> l, 1) << l
        for i in range(1 << l):
            send_ref[first + i] = block
    send_ref[own] = jnp.zeros((rhs, rank), jnp.float32)


def head(scal, order, charges, points, basis):
    levels, leaf, rank = basis.shape
    rhs = charges.shape[0]
    vmem = pl.BlockSpec(memory_space=pltpu.VMEM)
    hbm = pl.BlockSpec(memory_space=pltpu.HBM)
    return pl.pallas_call(
        head_kernel,
        in_specs=[pl.BlockSpec(memory_space=pltpu.SMEM), hbm, hbm, hbm, hbm],
        out_specs=[vmem, vmem, vmem, vmem],
        out_shape=[
            jax.ShapeDtypeStruct((rhs, leaf), jnp.bfloat16),
            pltpu.VMEM((1 << levels, rhs, rank), jnp.float32),
            jax.ShapeDtypeStruct((leaf, 32), jnp.bfloat16),
            jax.ShapeDtypeStruct((32, leaf), jnp.bfloat16),
        ],
        scratch_shapes=[
            pltpu.VMEM(basis.shape, basis.dtype),
            pltpu.VMEM(order.shape, order.dtype),
            pltpu.VMEM(charges.shape, charges.dtype),
            pltpu.VMEM(points.shape, points.dtype),
            pltpu.VMEM((leaf // 128 * rhs, 128), jnp.bfloat16),
            pltpu.VMEM((rhs, levels * rank), jnp.float32),
            pltpu.VMEM((8, leaf), jnp.float32),
            pltpu.SemaphoreType.DMA((leaf // min(512, leaf) + 3,)),
        ],
        compiler_params=pltpu.CompilerParams(vmem_limit_bytes=24 << 20),
        name="head",
    )(scal, *[in_hbm(x) for x in (order, charges, points, basis)])


def near_kernel(scal_ref, tall_ref, wide_ref, live_ref, skel_ref, near_ref, coup_ref):
    rhs, leaf = live_ref.shape
    columns = min(2048, leaf)
    rows = min(512, leaf)
    own = scal_ref[1]
    devices = 1 << coup_ref.shape[0]
    for l in range(coup_ref.shape[0]):
        node = (devices + own) >> l
        gap = None
        for axis in range(3):
            mine = skel_ref[axis, pl.ds(node, 1), :]
            other = skel_ref[axis, pl.ds(jnp.bitwise_xor(node, 1), 1), :]
            other = jnp.broadcast_to(other, (other.shape[1], other.shape[1])).T
            diff = other - mine
            gap = diff * diff if gap is None else gap + diff * diff
        coup_ref[l] = jnp.exp2(gap * -log2_rate).astype(jnp.bfloat16)

    def column_block(step, carry):
        first = pl.multiple_of(step * columns, 128)
        column = wide_ref[:, pl.ds(first, columns)]
        total = jnp.zeros((rhs, columns), jnp.float32)
        for at in range(0, leaf, rows):
            power = jnp.dot(tall_ref[at : at + rows, :], column, preferred_element_type=jnp.float32)
            kernel = jnp.exp2(power).astype(jnp.bfloat16)
            total += jnp.dot(live_ref[:, at : at + rows], kernel, preferred_element_type=jnp.float32)
        near_ref[:, pl.ds(first, columns)] = total
        return carry

    lax.fori_loop(0, leaf // columns, column_block, 0)


def near(scal, tall, wide, live, skeletons, levels):
    rhs, leaf = live.shape
    rank = skeletons.shape[2]
    vmem = pl.BlockSpec(memory_space=pltpu.VMEM)
    return pl.pallas_call(
        near_kernel,
        in_specs=[pl.BlockSpec(memory_space=pltpu.SMEM), vmem, vmem, vmem, vmem],
        out_specs=[vmem, vmem],
        out_shape=[
            jax.ShapeDtypeStruct((rhs, leaf), jnp.float32),
            jax.ShapeDtypeStruct((levels, rank, rank), jnp.bfloat16),
        ],
        compiler_params=pltpu.CompilerParams(vmem_limit_bytes=24 << 20),
        cost_estimate=pl.CostEstimate(flops=4 << 30, bytes_accessed=1 << 20, transcendentals=leaf * leaf),
        name="near",
    )(scal, tall, wide, live, skeletons)


def tail_kernel(scal_ref, got_ref, coup_ref, near_ref, basis_hbm, out_ref, basis_ref, coupled_ref, sems):
    levels, leaf, rank = basis_ref.shape
    rhs = near_ref.shape[0]
    rows = min(512, leaf)
    copies = [
        pltpu.make_async_copy(
            basis_hbm.at[:, pl.ds(s * rows, rows), :], basis_ref.at[:, pl.ds(s * rows, rows), :], sems.at[s]
        )
        for s in range(leaf // rows)
    ]
    for copy in copies:
        copy.start()
    own = scal_ref[1]
    for l in range(levels):
        first = jnp.bitwise_xor(own >> l, 1) << l
        sums = [got_ref[first + i] for i in range(1 << l)]
        while len(sums) > 1:
            sums = [a + b for a, b in zip(sums[::2], sums[1::2])]
        coupled = jnp.dot(sums[0].astype(jnp.bfloat16), coup_ref[l], preferred_element_type=jnp.float32)
        coupled_ref[:, l * rank : (l + 1) * rank] = coupled.astype(jnp.bfloat16)
    for s in range(leaf // rows):
        at = s * rows
        copies[s].wait()
        basis = jnp.concatenate([basis_ref[l, at : at + rows, :] for l in range(levels)], axis=1)
        far = lax.dot_general(
            coupled_ref[...], basis, (((1,), (1,)), ((), ())), preferred_element_type=jnp.float32
        )
        field = dense_gain / math.sqrt(leaf) * near_ref[:, at : at + rows] + far * (expand_gain / math.sqrt(rank))
        slot = lax.broadcasted_iota(jnp.int32, (rhs, rows), 1) + at
        out_ref[:, at : at + rows] = jnp.where(slot < scal_ref[0], field, 0.0)


def tail(scal, got, coup, near_field, basis):
    levels, leaf, rank = basis.shape
    rhs = near_field.shape[0]
    rows = min(512, leaf)
    vmem = pl.BlockSpec(memory_space=pltpu.VMEM)
    return pl.pallas_call(
        tail_kernel,
        in_specs=[pl.BlockSpec(memory_space=pltpu.SMEM), vmem, vmem, vmem, pl.BlockSpec(memory_space=pltpu.HBM)],
        out_specs=vmem,
        out_shape=jax.ShapeDtypeStruct((rhs, leaf), jnp.float32),
        scratch_shapes=[
            pltpu.VMEM(basis.shape, basis.dtype),
            pltpu.VMEM((rhs, levels * rank), jnp.bfloat16),
            pltpu.SemaphoreType.DMA((leaf // rows,)),
        ],
        compiler_params=pltpu.CompilerParams(vmem_limit_bytes=24 << 20),
        name="tail",
    )(scal, got, coup, near_field, in_hbm(basis))


def per_device(points, charges, arrival_order, counts, basis_rows, skeletons):
    scal = jnp.stack([counts[0], device_index()])
    live, send, tall, wide = head(scal, arrival_order, charges, points, basis_rows)
    got = lax.all_to_all(send, axes, 0, 0, tiled=True)
    near_field, coup = near(scal, tall, wide, live, skeletons, basis_rows.shape[0])
    return tail(scal, got, coup, near_field, basis_rows)


def solution(mesh):
    placed = (
        P(None, axes),
        P(None, axes),
        P(axes, None),
        P(axes),
        P(None, axes, None),
        P(),
    )
    return jax.shard_map(
        per_device,
        mesh=mesh,
        in_specs=placed,
        out_specs=P(None, axes),
        check_vma=False,
    )
```

time: 91.1 us -> 37.2 us (0.41)
  the two profiles are of different devices: /device:TPU:12 before, /device:TPU:1 now
where the time goes in v2:
time: 37.2 us; the launch traced here: 37.1 us
  Pallas kernels  24.8 us (67%)
  starting transfers between devices  11.5 us (31%)
  between operations  0.73 us (2%)
    pallas_call x1, Pallas kernels, near(): pl.pallas_call(near_kernel, in_specs=[pl.BlockSpec(memory_space=pltpu.SME...  14.1 us
    all_to_all x1, starting transfers between devices, per_device(): got = lax.all_to_all(send, axes, 0, 0, tiled=True)  11.5 us
    pallas_call x1, Pallas kernels, head(): pl.pallas_call(head_kernel, in_specs=[pl.BlockSpec(memory_space=pltpu.SME...  5.37 us
    pallas_call x1, Pallas kernels, tail(): pl.pallas_call(tail_kernel, in_specs=[pl.BlockSpec(memory_space=pltpu.SME...  5.35 us
  transfers between devices with their start and end apart: 1, of which 0 were waited for; matrix products, arithmetic and copies ran while one was open for 0% of the time, Pallas kernels for 38%

profile of v2, /device:TPU:1, one launch (start us, length us, event | category | flops | bytes accessed | tf_op | source)
XLA Modules:
  0.0 37.1 jit_solution(4786584312064867575)
XLA Ops:
  0.0 0.0 copy-start
  0.7 0.1 pad_add_fusion.scal_ref
  0.8 5.4 %head.1 = (bf16[8,4096]{1,0:T(8,128)(2,1)S(1)}, f32[128,8,128]{2,1,0:T(8,128)}, bf16[4096,32]{1,0:T(8,128)(2,1)S(1)}, bf16[32,4096]{1,0:T(8,128)(2,1)S(1)}) custom-call(s32[2]{0:T(128)S(1)} %pad_add_fusion.scal_ref, s32[1,4096]{1,0:T(1,128)} %order_hbm.1, bf16[8,4096]{1,0:T(8,128)(2,1)} %charges_hbm.1, f32[3,4096]{1,0:T(4,128)} %points_hbm.1, ...), custom_call_target="tpu_custom_call" | custom-call | tf_op jit(solution)/shard_map/head/pallas_call | solution.py:121
  6.2 11.5 %all-to-all-start = ((f32[128,8,128]{2,1,0:T(8,128)}), f32[128,8,128]{2,1,0:T(8,128)S(1)}, u32[]{:S(2)}, u32[]{:S(2)}) async-start(f32[128,8,128]{2,1,0:T(8,128)} %get-tuple-element.11), calls=%async_computation | async-start | bytes 1048576 | tf_op jit(solution)/shard_map/all_to_all | solution.py:250
  17.7 0.0 copy-done
  17.7 14.1 %near.1 = (f32[8,4096]{1,0:T(8,128)S(1)}, bf16[7,128,128]{2,1,0:T(8,128)(2,1)S(1)}) custom-call(s32[2]{0:T(128)S(1)} %pad_add_fusion.scal_ref, bf16[4096,32]{1,0:T(8,128)(2,1)S(1)} %get-tuple-element.12.tall_ref, bf16[32,4096]{1,0:T(8,128)(2,1)S(1)} %get-tuple-element.13.wide_ref, bf16[8,4096]{1,0:T(8,128)(2,1)S(1)} %get-tuple-element.14.live_ref, ...), custom_call_target="tpu_custom_call" | custom-call | flops 4294967296 | bytes 1048576 | tf_op jit(solution)/shard_map/near/pallas_call | solution.py:181
  31.7 0.0 all-to-all-done.got_ref
  31.7 5.3 %tail.1 = f32[8,4096]{1,0:T(8,128)} custom-call(s32[2]{0:T(128)S(1)} %pad_add_fusion.scal_ref, f32[128,8,128]{2,1,0:T(8,128)S(1)} %all-to-all-done.got_ref, bf16[7,128,128]{2,1,0:T(8,128)(2,1)S(1)} %get-tuple-element.15.coup_ref, f32[8,4096]{1,0:T(8,128)S(1)} %get-tuple-element.16.near_ref, bf16[7,4096,128]{2,1,0:T(8,128)(2,1)} %basis_hbm.3), custom_call_target="tpu_custom_call" | custom-call | tf_op jit(solution)/shard_map/tail/pallas_call | solution.py:232
Async XLA Ops:
  0.0 17.7 %copy-start = (f32[3,256,128]{2,1,0:T(8,128)S(1)}, f32[3,256,128]{2,1,0:T(8,128)}, u32[]{:S(2)}) copy-start(f32[3,256,128]{2,1,0:T(8,128)} %skel_ref.1) | copy-start | bytes 1179652
  6.2 25.6 %all-to-all-start = ((f32[128,8,128]{2,1,0:T(8,128)}), f32[128,8,128]{2,1,0:T(8,128)S(1)}, u32[]{:S(2)}, u32[]{:S(2)}) async-start(f32[128,8,128]{2,1,0:T(8,128)} %get-tuple-element.11), calls=%async_computation | async-start | bytes 1048576 | tf_op jit(solution)/shard_map/all_to_all | solution.py:250

commit v3 on v2

--- a/solution.py
+++ b/solution.py
@@ -49,19 +49,21 @@
     tall = [jnp.where(axis, high, place), jnp.where(axis, mid, ones), high, mid]
     wide_ref[...] = jnp.concatenate(wide, axis=0).astype(jnp.bfloat16)
     tall = jnp.concatenate(tall, axis=0)
-    for b in range(leaf // 128):
-        tall_ref[b * 128 : (b + 1) * 128, :] = tall[:, b * 128 : (b + 1) * 128].T.astype(jnp.bfloat16)
+    side = leaf // 4
+    for at in range(0, side, 128):
+        quarters = [tall[:, g * side + at : g * side + at + 128] for g in range(4)]
+        tall_ref[at : at + 128, :] = jnp.concatenate(quarters, axis=0).T.astype(jnp.bfloat16)
 
 
 def head_kernel(
     scal_ref, order_hbm, charges_hbm, points_hbm, basis_hbm,
-    live_ref, send_ref, tall_ref, wide_ref,
+    live_ref, proj_ref, tall_ref, wide_ref,
     basis_ref, order_ref, charges_ref, points_ref, table_ref, acc_ref, spare_ref, sems,
 ):
     levels, leaf, rank = basis_ref.shape
     rhs = charges_ref.shape[0]
     high = leaf // 128
-    rows = min(512, leaf)
+    rows = min(1024, leaf)
     steps = leaf // rows
     small = [
         pltpu.make_async_copy(charges_hbm, charges_ref, sems.at[steps]),
@@ -103,14 +105,9 @@
         live = live_ref[:, s * rows : (s + 1) * rows]
         basis = jnp.concatenate([basis_ref[l, s * rows : (s + 1) * rows, :] for l in range(levels)], axis=1)
         acc_ref[...] += jnp.dot(live, basis, preferred_element_type=jnp.float32)
-    own = scal_ref[1]
     for l in range(levels):
         scale = 2.0 ** (-0.5 * l) / math.sqrt(leaf)
-        block = acc_ref[:, l * rank : (l + 1) * rank] * scale
-        first = jnp.bitwise_xor(own >> l, 1) << l
-        for i in range(1 << l):
-            send_ref[first + i] = block
-    send_ref[own] = jnp.zeros((rhs, rank), jnp.float32)
+        proj_ref[l] = acc_ref[:, l * rank : (l + 1) * rank] * scale
 
 
 def head(scal, order, charges, points, basis):
@@ -124,8 +121,8 @@
         out_specs=[vmem, vmem, vmem, vmem],
         out_shape=[
             jax.ShapeDtypeStruct((rhs, leaf), jnp.bfloat16),
-            pltpu.VMEM((1 << levels, rhs, rank), jnp.float32),
-            jax.ShapeDtypeStruct((leaf, 32), jnp.bfloat16),
+            jax.ShapeDtypeStruct((levels, rhs, rank), jnp.float32),
+            jax.ShapeDtypeStruct((leaf // 4, 128), jnp.bfloat16),
             jax.ShapeDtypeStruct((32, leaf), jnp.bfloat16),
         ],
         scratch_shapes=[
@@ -136,17 +133,31 @@
             pltpu.VMEM((leaf // 128 * rhs, 128), jnp.bfloat16),
             pltpu.VMEM((rhs, levels * rank), jnp.float32),
             pltpu.VMEM((8, leaf), jnp.float32),
-            pltpu.SemaphoreType.DMA((leaf // min(512, leaf) + 3,)),
+            pltpu.SemaphoreType.DMA((leaf // min(1024, leaf) + 3,)),
         ],
         compiler_params=pltpu.CompilerParams(vmem_limit_bytes=24 << 20),
         name="head",
     )(scal, *[in_hbm(x) for x in (order, charges, points, basis)])
 
 
-def near_kernel(scal_ref, tall_ref, wide_ref, live_ref, skel_ref, near_ref, coup_ref):
-    rhs, leaf = live_ref.shape
-    columns = min(2048, leaf)
-    rows = min(512, leaf)
+def near_blocks(tall_ref, wide_ref, live_ref, near_ref):
+    side = live_ref.shape[1] // 4
+    near_ref[...] = jnp.zeros_like(near_ref)
+    for row in range(4):
+        for col in range(row, 4):
+            own = slice(row * side, (row + 1) * side)
+            other = slice(col * side, (col + 1) * side)
+            column = [wide_ref[:, other] if g == row else jnp.zeros((32, side), jnp.bfloat16) for g in range(4)]
+            power = jnp.dot(tall_ref[...], jnp.concatenate(column, axis=0), preferred_element_type=jnp.float32)
+            kernel = jnp.exp2(power).astype(jnp.bfloat16)
+            near_ref[:, other] += jnp.dot(live_ref[:, own], kernel, preferred_element_type=jnp.float32)
+            if row != col:
+                near_ref[:, own] += lax.dot_general(
+                    live_ref[:, other], kernel, (((1,), (1,)), ((), ())), preferred_element_type=jnp.float32
+                )
+
+
+def couple_kernel(scal_ref, live_hbm, skel_ref, coup_ref):
     own = scal_ref[1]
     devices = 1 << coup_ref.shape[0]
     for l in range(coup_ref.shape[0]):
@@ -160,96 +171,137 @@
             gap = diff * diff if gap is None else gap + diff * diff
         coup_ref[l] = jnp.exp2(gap * -log2_rate).astype(jnp.bfloat16)
 
-    def column_block(step, carry):
-        first = pl.multiple_of(step * columns, 128)
-        column = wide_ref[:, pl.ds(first, columns)]
-        total = jnp.zeros((rhs, columns), jnp.float32)
-        for at in range(0, leaf, rows):
-            power = jnp.dot(tall_ref[at : at + rows, :], column, preferred_element_type=jnp.float32)
-            kernel = jnp.exp2(power).astype(jnp.bfloat16)
-            total += jnp.dot(live_ref[:, at : at + rows], kernel, preferred_element_type=jnp.float32)
-        near_ref[:, pl.ds(first, columns)] = total
-        return carry
-
-    lax.fori_loop(0, leaf // columns, column_block, 0)
-
-
-def near(scal, tall, wide, live, skeletons, levels):
+
+def couple(scal, live, skeletons, levels):
+    rank = skeletons.shape[2]
+    vmem = pl.BlockSpec(memory_space=pltpu.VMEM)
+    return pl.pallas_call(
+        couple_kernel,
+        in_specs=[pl.BlockSpec(memory_space=pltpu.SMEM), pl.BlockSpec(memory_space=pl.ANY), vmem],
+        out_specs=vmem,
+        out_shape=jax.ShapeDtypeStruct((levels, rank, rank), jnp.bfloat16),
+        compiler_params=pltpu.CompilerParams(vmem_limit_bytes=8 << 20),
+        cost_estimate=pl.CostEstimate(flops=1 << 20, bytes_accessed=1 << 19, transcendentals=1 << 17),
+        name="couple",
+    )(scal, live, skeletons)
+
+
+def pack_kernel(scal_ref, mine_ref, other_ref, send_ref):
+    own = scal_ref[1] >> 1
+    levels = mine_ref.shape[0]
+    for l in range(1, levels):
+        block = mine_ref[l] + other_ref[l]
+        first = jnp.bitwise_xor(own >> (l - 1), 1) << (l - 1)
+        for i in range(1 << (l - 1)):
+            send_ref[first + i] = block
+    send_ref[own] = jnp.zeros(mine_ref.shape[1:], jnp.float32)
+
+
+def pack(scal, mine, other):
+    vmem = pl.BlockSpec(memory_space=pltpu.VMEM)
+    return pl.pallas_call(
+        pack_kernel,
+        in_specs=[pl.BlockSpec(memory_space=pltpu.SMEM), vmem, vmem],
+        out_specs=vmem,
+        out_shape=jax.ShapeDtypeStruct((1 << (mine.shape[0] - 1), *mine.shape[1:]), jnp.float32),
+        compiler_params=pltpu.CompilerParams(vmem_limit_bytes=8 << 20),
+        name="pack",
+    )(scal, mine, other)
+
+
+def near_kernel(tall_ref, wide_ref, live_ref, send_hbm, basis_hbm, near_ref, kept_ref, sem):
+    held = kept_ref.shape[0]
+    copy = pltpu.make_async_copy(basis_hbm.at[pl.ds(basis_hbm.shape[0] - held, held)], kept_ref, sem)
+    copy.start()
+    near_blocks(tall_ref, wide_ref, live_ref, near_ref)
+    copy.wait()
+
+
+def near(tall, wide, live, send, basis, held):
     rhs, leaf = live.shape
-    rank = skeletons.shape[2]
     vmem = pl.BlockSpec(memory_space=pltpu.VMEM)
     return pl.pallas_call(
         near_kernel,
-        in_specs=[pl.BlockSpec(memory_space=pltpu.SMEM), vmem, vmem, vmem, vmem],
+        in_specs=[vmem, vmem, vmem, pl.BlockSpec(memory_space=pl.ANY), pl.BlockSpec(memory_space=pltpu.HBM)],
         out_specs=[vmem, vmem],
         out_shape=[
             jax.ShapeDtypeStruct((rhs, leaf), jnp.float32),
-            jax.ShapeDtypeStruct((levels, rank, rank), jnp.bfloat16),
+            pltpu.VMEM((held, *basis.shape[1:]), basis.dtype),
         ],
+        scratch_shapes=[pltpu.SemaphoreType.DMA(())],
         compiler_params=pltpu.CompilerParams(vmem_limit_bytes=24 << 20),
         cost_estimate=pl.CostEstimate(flops=4 << 30, bytes_accessed=1 << 20, transcendentals=leaf * leaf),
         name="near",
-    )(scal, tall, wide, live, skeletons)
-
-
-def tail_kernel(scal_ref, got_ref, coup_ref, near_ref, basis_hbm, out_ref, basis_ref, coupled_ref, sems):
-    levels, leaf, rank = basis_ref.shape
+    )(tall, wide, live, send, in_hbm(basis))
+
+
+def tail_kernel(
+    scal_ref, other_ref, got_ref, coup_ref, near_ref, kept_ref, basis_hbm, out_ref, basis_ref, coupled_ref, sems
+):
+    fetched, leaf, rank = basis_ref.shape
+    levels = fetched + kept_ref.shape[0]
     rhs = near_ref.shape[0]
-    rows = min(512, leaf)
-    copies = [
-        pltpu.make_async_copy(
-            basis_hbm.at[:, pl.ds(s * rows, rows), :], basis_ref.at[:, pl.ds(s * rows, rows), :], sems.at[s]
-        )
-        for s in range(leaf // rows)
-    ]
+    copies = [pltpu.make_async_copy(basis_hbm.at[l], basis_ref.at[l], sems.at[l]) for l in range(fetched)]
     for copy in copies:
         copy.start()
-    own = scal_ref[1]
+    own = scal_ref[1] >> 1
     for l in range(levels):
-        first = jnp.bitwise_xor(own >> l, 1) << l
-        sums = [got_ref[first + i] for i in range(1 << l)]
+        if l == 0:
+            sums = [other_ref[0]]
+        else:
+            first = jnp.bitwise_xor(own >> (l - 1), 1) << (l - 1)
+            sums = [got_ref[first + i] for i in range(1 << (l - 1))]
         while len(sums) > 1:
             sums = [a + b for a, b in zip(sums[::2], sums[1::2])]
         coupled = jnp.dot(sums[0].astype(jnp.bfloat16), coup_ref[l], preferred_element_type=jnp.float32)
         coupled_ref[:, l * rank : (l + 1) * rank] = coupled.astype(jnp.bfloat16)
-    for s in range(leaf // rows):
-        at = s * rows
-        copies[s].wait()
-        basis = jnp.concatenate([basis_ref[l, at : at + rows, :] for l in range(levels)], axis=1)
+    out_ref[...] = near_ref[...] * (dense_gain / math.sqrt(leaf))
+    parts = [range(fetched, levels)] + [range(l, min(l + 2, fetched)) for l in range(0, fetched, 2)]
+    for part in parts:
+        rows = []
+        for l in part:
+            if l < fetched:
+                copies[l].wait()
+            rows.append(basis_ref[l] if l < fetched else kept_ref[l - fetched])
+        coupled = coupled_ref[:, part[0] * rank : (part[-1] + 1) * rank]
         far = lax.dot_general(
-            coupled_ref[...], basis, (((1,), (1,)), ((), ())), preferred_element_type=jnp.float32
+            coupled, jnp.concatenate(rows, axis=1), (((1,), (1,)), ((), ())), preferred_element_type=jnp.float32
         )
-        field = dense_gain / math.sqrt(leaf) * near_ref[:, at : at + rows] + far * (expand_gain / math.sqrt(rank))
-        slot = lax.broadcasted_iota(jnp.int32, (rhs, rows), 1) + at
-        out_ref[:, at : at + rows] = jnp.where(slot < scal_ref[0], field, 0.0)
-
-
-def tail(scal, got, coup, near_field, basis):
+        out_ref[...] += far * (expand_gain / math.sqrt(rank))
+    slot = lax.broadcasted_iota(jnp.int32, (rhs, leaf), 1)
+    out_ref[...] = jnp.where(slot < scal_ref[0], out_ref[...], 0.0)
+
+
+def tail(scal, other, got, coup, near_field, kept, basis):
     levels, leaf, rank = basis.shape
     rhs = near_field.shape[0]
-    rows = min(512, leaf)
     vmem = pl.BlockSpec(memory_space=pltpu.VMEM)
     return pl.pallas_call(
         tail_kernel,
-        in_specs=[pl.BlockSpec(memory_space=pltpu.SMEM), vmem, vmem, vmem, pl.BlockSpec(memory_space=pltpu.HBM)],
+        in_specs=[pl.BlockSpec(memory_space=pltpu.SMEM)] + [vmem] * 5 + [pl.BlockSpec(memory_space=pltpu.HBM)],
         out_specs=vmem,
         out_shape=jax.ShapeDtypeStruct((rhs, leaf), jnp.float32),
         scratch_shapes=[
-            pltpu.VMEM(basis.shape, basis.dtype),
+            pltpu.VMEM((levels - kept.shape[0], leaf, rank), basis.dtype),
             pltpu.VMEM((rhs, levels * rank), jnp.bfloat16),
-            pltpu.SemaphoreType.DMA((leaf // rows,)),
+            pltpu.SemaphoreType.DMA((levels - kept.shape[0],)),
         ],
         compiler_params=pltpu.CompilerParams(vmem_limit_bytes=24 << 20),
         name="tail",
-    )(scal, got, coup, near_field, in_hbm(basis))
+    )(scal, other, got, coup, near_field, kept, in_hbm(basis))
 
 
 def per_device(points, charges, arrival_order, counts, basis_rows, skeletons):
     scal = jnp.stack([counts[0], device_index()])
-    live, send, tall, wide = head(scal, arrival_order, charges, points, basis_rows)
-    got = lax.all_to_all(send, axes, 0, 0, tiled=True)
-    near_field, coup = near(scal, tall, wide, live, skeletons, basis_rows.shape[0])
-    return tail(scal, got, coup, near_field, basis_rows)
+    live, mine, tall, wide = head(scal, arrival_order, charges, points, basis_rows)
+    count = 1 << basis_rows.shape[0]
+    other = lax.ppermute(mine, axes, [(d, d ^ 1) for d in range(count)])
+    coup = couple(scal, live, skeletons, basis_rows.shape[0])
+    send = pack(scal, mine, other)
+    chips = [list(range(core, count, 2)) for core in range(2)]
+    got = lax.all_to_all(send, axes, 0, 0, axis_index_groups=chips, tiled=True)
+    near_field, kept = near(tall, wide, live, send, basis_rows, 2)
+    return tail(scal, other, got, coup, near_field, kept, basis_rows)
 
 
 def solution(mesh):

time: 37.2 us -> 36.5 us (0.981)
  Pallas kernels: 24.8 us -> 22.5 us
  starting transfers between devices: 11.5 us -> 12.9 us
    ppermute x0 -> x1, starting transfers between devices: none -> 1.46 us  [per_device(): other = lax.ppermute(mine, axes, [(d, d ^ 1) for d in range(count)])]
    pallas_call x1, Pallas kernels: 5.37 us -> 4.22 us  [head(): pl.pallas_call(head_kernel, in_specs=[pl.BlockSpec(memory_space=pltpu.SME...]
    pallas_call x1, Pallas kernels: 5.35 us -> 4.64 us  [tail(): pl.pallas_call(tail_kernel, in_specs=[pl.BlockSpec(memory_space=pltpu.SME...]
    pallas_call x1 -> x3, Pallas kernels: 14.1 us -> 13.6 us  [the longest x1 11.4 us: near(): pl.pallas_call(near_kernel, in_specs=[vmem, vmem, vmem, pl.BlockSpec(memo...]
  transfers between devices with their start and end apart: 1 -> 2, of which waited for: 0 -> 0; matrix products, arithmetic and copies ran while one was open for 0% -> 0% of each run, Pallas kernels for 38% -> 34%
where the time goes in v3:
time: 36.5 us; the launch traced here: 36.4 us
  Pallas kernels  22.5 us (62%)
  starting transfers between devices  12.9 us (35%)
  between operations  0.91 us (2%)
    all_to_all x1, starting transfers between devices, per_device(): got = lax.all_to_all(send, axes, 0, 0, axis_index_groups=chips, tiled=True)  11.4 us
    pallas_call x1, Pallas kernels, near(): pl.pallas_call(near_kernel, in_specs=[vmem, vmem, vmem, pl.BlockSpec(memo...  11.4 us
    pallas_call x1, Pallas kernels, tail(): pl.pallas_call(tail_kernel, in_specs=[pl.BlockSpec(memory_space=pltpu.SME...  4.64 us
    pallas_call x1, Pallas kernels, head(): pl.pallas_call(head_kernel, in_specs=[pl.BlockSpec(memory_space=pltpu.SME...  4.22 us
    ppermute x1, starting transfers between devices, per_device(): other = lax.ppermute(mine, axes, [(d, d ^ 1) for d in range(count)])  1.46 us
    pallas_call x1, Pallas kernels, pack(): pl.pallas_call(pack_kernel, in_specs=[pl.BlockSpec(memory_space=pltpu.SME...  1.26 us
    pallas_call x1, Pallas kernels, couple(): pl.pallas_call(couple_kernel, in_specs=[pl.BlockSpec(memory_space=pltpu.S...  0.99 us
  transfers between devices with their start and end apart: 2, of which 0 were waited for; matrix products, arithmetic and copies ran while one was open for 0% of the time, Pallas kernels for 34%

profile of v3, /device:TPU:1, one launch (start us, length us, event | category | flops | bytes accessed | tf_op | source)
XLA Modules:
  0.0 36.4 jit_solution(287812856094666308)
XLA Ops:
  0.0 0.0 copy-start
  0.7 0.1 pad_add_fusion.scal_ref
  0.8 4.2 %head.1 = (bf16[8,4096]{1,0:T(8,128)(2,1)S(1)}, f32[7,8,128]{2,1,0:T(8,128)S(1)}, bf16[1024,128]{1,0:T(8,128)(2,1)S(1)}, bf16[32,4096]{1,0:T(8,128)(2,1)S(1)}) custom-call(s32[2]{0:T(128)S(1)} %pad_add_fusion.scal_ref, s32[1,4096]{1,0:T(1,128)} %order_hbm.1, bf16[8,4096]{1,0:T(8,128)(2,1)} %charges_hbm.1, f32[3,4096]{1,0:T(4,128)} %points_hbm.1, ...), custom_call_target="tpu_custom_call" | custom-call | tf_op jit(solution)/shard_map/head/pallas_call | solution.py:118
  5.0 1.5 %collective-permute-start = (f32[7,8,128]{2,1,0:T(8,128)S(1)}, f32[7,8,128]{2,1,0:T(8,128)S(1)}, u32[]{:S(2)}, u32[]{:S(2)}) collective-permute-start(f32[7,8,128]{2,1,0:T(8,128)S(1)} %get-tuple-element.11.mine_ref), channel_id=1, source_target_pairs={{0,1},{1,0},{2,3},{3,2},{4,5},{5,4},{6,7},{7,6},{8,9},{9,8},{10,11... | collective-permute-start | bytes 86024 | tf_op jit(solution)/shard_map/ppermute | solution.py:298
  6.5 0.0 copy-done
  6.5 1.0 %couple.1.coup_ref = bf16[7,128,128]{2,1,0:T(8,128)(2,1)S(1)} custom-call(s32[2]{0:T(128)S(1)} %pad_add_fusion.scal_ref, bf16[8,4096]{1,0:T(8,128)(2,1)S(1)} %get-tuple-element.12.live_hbm.live_ref, f32[3,256,128]{2,1,0:T(8,128)S(1)} %copy-done), custom_call_target="tpu_custom_call" | custom-call | flops 1048576 | bytes 524288 | tf_op jit(solution)/shard_map/couple/pallas_call | solution.py:178
  7.5 0.0 collective-permute-done.other_ref
  7.5 1.3 %pack.1.send_hbm = f32[64,8,128]{2,1,0:T(8,128)} custom-call(s32[2]{0:T(128)S(1)} %pad_add_fusion.scal_ref, f32[7,8,128]{2,1,0:T(8,128)S(1)} %get-tuple-element.11.mine_ref, f32[7,8,128]{2,1,0:T(8,128)S(1)} %collective-permute-done.other_ref), custom_call_target="tpu_custom_call" | custom-call | tf_op jit(solution)/shard_map/pack/pallas_call | solution.py:202
  8.7 11.4 %all-to-all-start = ((f32[64,8,128]{2,1,0:T(8,128)}), f32[64,8,128]{2,1,0:T(8,128)S(1)}, u32[]{:S(2)}, u32[]{:S(2)}) async-start(f32[64,8,128]{2,1,0:T(8,128)} %pack.1.send_hbm), calls=%async_computation | async-start | bytes 524288 | tf_op jit(solution)/shard_map/all_to_all | solution.py:302
  20.2 11.4 %near.1 = (f32[8,4096]{1,0:T(8,128)S(1)}, bf16[2,4096,128]{2,1,0:T(8,128)(2,1)S(1)}) custom-call(bf16[1024,128]{1,0:T(8,128)(2,1)S(1)} %get-tuple-element.13.tall_ref, bf16[32,4096]{1,0:T(8,128)(2,1)S(1)} %get-tuple-element.14.wide_ref, bf16[8,4096]{1,0:T(8,128)(2,1)S(1)} %get-tuple-element.12.live_hbm.live_ref, f32[64,8,128]{2,1,0:T(8,128)} %pack.1.send_hbm, ...), custom_call_target="tpu_custom_call" | custom-call | flops 4294967296 | bytes 1048576 | tf_op jit(solution)/shard_map/near/pallas_call | solution.py:223
  31.5 0.0 all-to-all-done.got_ref
  31.6 4.6 %tail.1 = f32[8,4096]{1,0:T(8,128)} custom-call(s32[2]{0:T(128)S(1)} %pad_add_fusion.scal_ref, f32[7,8,128]{2,1,0:T(8,128)S(1)} %collective-permute-done.other_ref, f32[64,8,128]{2,1,0:T(8,128)S(1)} %all-to-all-done.got_ref, bf16[7,128,128]{2,1,0:T(8,128)(2,1)S(1)} %couple.1.coup_ref, f32[8,4096]{1,0:T(8,128)S(1)} %get-tuple-element.15.near_ref, ...), custom_call_target="tpu_custom_call" | custom-call | tf_op jit(solution)/shard_map/tail/pallas_call | solution.py:279
Async XLA Ops:
  0.0 6.5 %copy-start = (f32[3,256,128]{2,1,0:T(8,128)S(1)}, f32[3,256,128]{2,1,0:T(8,128)}, u32[]{:S(2)}) copy-start(f32[3,256,128]{2,1,0:T(8,128)} %skel_ref.1) | copy-start | bytes 1179652
  5.0 2.5 %collective-permute-start = (f32[7,8,128]{2,1,0:T(8,128)S(1)}, f32[7,8,128]{2,1,0:T(8,128)S(1)}, u32[]{:S(2)}, u32[]{:S(2)}) collective-permute-start(f32[7,8,128]{2,1,0:T(8,128)S(1)} %get-tuple-element.11.mine_ref), channel_id=1, source_target_pairs={{0,1},{1,0},{2,3},{3,2},{4,5},{5,4},{6,7},{7,6},{8,9},{9,8},{10,11... | collective-permute-start | bytes 86024 | tf_op jit(solution)/shard_map/ppermute | solution.py:298
  8.7 22.8 %all-to-all-start = ((f32[64,8,128]{2,1,0:T(8,128)}), f32[64,8,128]{2,1,0:T(8,128)S(1)}, u32[]{:S(2)}, u32[]{:S(2)}) async-start(f32[64,8,128]{2,1,0:T(8,128)} %pack.1.send_hbm), calls=%async_computation | async-start | bytes 524288 | tf_op jit(solution)/shard_map/all_to_all | solution.py:302
